TPU v7x, 32 devices: a whole 2x2x4 slice. The times are simulated.
32 devices in a mesh: seq: 8 (over z, y), head: 4 (over x, core).
Axes of the slice: x: 2, y: 2, z: 4, core: 2. Of those that a mesh axis runs over, the one named last changes fastest.
Arguments:
- q_low: bfloat16 [2048, 1536], P('seq', 'head'), may hold values from -500 to 500
- q_gain: bfloat16 [1536], P('head'), may hold values from 0.099609375 to 1.8984375
- q_up: bfloat16 [1536, 24576], P(None, 'head'), may hold values from -0.15625 to 0.15625
- key_absorb: bfloat16 [128, 128, 512], P('head'), may hold values from -0.5 to 0.5
- value_absorb: bfloat16 [128, 512, 128], P('head'), may hold values from -0.25 to 0.25
- latent_cache: bfloat16 [65536, 576], P('seq'), may hold values from -1300 to 1300
- tile_picks: int32 [16, 16], P('seq'), may hold values from 0 to 511, as said below
Outputs:
- attended: bfloat16 [2048, 16384], P('seq', 'head')
Inputs may be any that keep to these rules, and one draw needn't show every extreme that they name: `tile_picks`: the 16 tiles of one query block differ. Of all tiles that the query blocks of one index of seq select together, at most 8 lie in the cache rows of one index of seq, and exactly 8 in those of some index.
All inputs are finite; a program needn't handle non-finite values.
Results may differ from a plain program's by a relative error of at most 0.03.
Values may be sent and summed in bfloat16 or wider, within the bound.
A program may use at most 192 MiB of HBM per device.

v0:
```python
import jax
import jax.numpy as jnp
from jax import lax
from jax.sharding import PartitionSpec as P

NOPE = 128
ROPE = 64
LATENT = 512
VDIM = 128
TILE = 128
TOPT = 16
QBLK = 128


def rms_normed(q_low, q_gain):
    values = q_low.astype(jnp.float32)
    power = jnp.mean(values * values, axis=-1, keepdims=True)
    return (values * lax.rsqrt(power + 1e-06) * q_gain.astype(jnp.float32)).astype(jnp.bfloat16)


def rotate(rope, positions):
    half = rope.shape[-1] // 2
    freq = jnp.power(
        jnp.float32(10000.0), -(2.0 * jnp.arange(half, dtype=jnp.float32)) / rope.shape[-1]
    )
    angle = positions.astype(jnp.float32)[:, None] * freq[None, :]
    cosine = jnp.cos(angle)[:, None, :]
    sine = jnp.sin(angle)[:, None, :]
    first = rope[..., :half].astype(jnp.float32)
    second = rope[..., half:].astype(jnp.float32)
    return jnp.concatenate(
        [first * cosine - second * sine, first * sine + second * cosine], axis=-1
    ).astype(jnp.bfloat16)


def owner_rank(picks, tiles_dev):
    owner = picks // tiles_dev
    order = jnp.arange(picks.shape[0], dtype=jnp.int32)
    before = (owner[:, None] == owner[None, :]) & (order[None, :] < order[:, None])
    return (owner, jnp.sum(before.astype(jnp.int32), axis=1))


def place_table(place, local, length):
    hit = place[:, None] == jnp.arange(length, dtype=jnp.int32)[None, :]
    return jnp.sum(jnp.where(hit, local[:, None], 0), axis=0)


def body(q_low, q_gain, q_up, key_absorb, value_absorb, latent_cache, tile_picks):
    whole_low, whole_gain = (
        lax.all_gather(q_low, "head", axis=1, tiled=True),
        lax.all_gather(q_gain, "head", axis=0, tiled=True),
    )
    rows = whole_low.shape[0]
    group = key_absorb.shape[0]
    width = latent_cache.shape[1]
    seq_count = lax.axis_size("seq")
    tiles_dev = latent_cache.shape[0] // TILE
    picks = tile_picks.reshape(-1)
    count = picks.shape[0]
    cap = max(2, 2 * count // seq_count)
    owner, rank = owner_rank(picks, tiles_dev)
    cache_tiles = latent_cache.reshape(tiles_dev, TILE, width)
    share = TILE // lax.axis_size("head")
    cache_tiles = lax.dynamic_slice_in_dim(cache_tiles, lax.axis_index("head") * share, share, 1)
    requests = place_table(owner * cap + rank, picks % tiles_dev, seq_count * cap).reshape(
        seq_count, cap
    )
    serve_requests = lax.all_to_all(requests, "seq", split_axis=0, concat_axis=0, tiled=True)
    found = jnp.take(cache_tiles, serve_requests, axis=0)
    fetched = lax.all_to_all(found, "seq", split_axis=0, concat_axis=0, tiled=True)
    flat = fetched.reshape(seq_count * cap, fetched.shape[2], width)
    keys = jnp.take(flat, owner * cap + rank, axis=0)
    keys = lax.all_gather(keys, "head", axis=1, tiled=True)
    keys = keys.reshape(count // TOPT, TOPT * TILE, width)
    normed = rms_normed(whole_low, whole_gain)
    query = jnp.dot(normed, q_up, preferred_element_type=jnp.float32).astype(jnp.bfloat16)
    query = query.reshape(rows, group, NOPE + ROPE)
    context = latent_cache.shape[0] * seq_count
    positions = context + lax.axis_index("seq") * rows + jnp.arange(rows, dtype=jnp.int32)
    rotated = rotate(query[..., NOPE:], positions)
    latent_q = jnp.einsum(
        "thn,hnl->thl", query[..., :NOPE], key_absorb, preferred_element_type=jnp.float32
    ).astype(jnp.bfloat16)
    full_q = jnp.concatenate([latent_q, rotated], axis=-1).reshape(
        count // TOPT, QBLK * group, width
    )
    scale = float(NOPE + ROPE) ** (-0.5)

    def one_block(operands):
        block_q, block_keys = operands
        scores = (
            lax.dot_general(
                block_q, block_keys, (((1,), (1,)), ((), ())), preferred_element_type=jnp.float32
            )
            * scale
        )
        weights = jax.nn.softmax(scores, axis=-1).astype(jnp.bfloat16)
        return jnp.dot(weights, block_keys[:, :LATENT], preferred_element_type=jnp.float32).astype(
            jnp.bfloat16
        )

    mixed = lax.map(one_block, (full_q, keys)).reshape(rows, group, LATENT)
    attended = jnp.einsum("thl,hlv->thv", mixed, value_absorb, preferred_element_type=jnp.float32)
    return attended.astype(jnp.bfloat16).reshape(rows, group * VDIM)


def solution(mesh):
    in_specs = (
        P("seq", "head"),
        P("head"),
        P(None, "head"),
        P("head", None, None),
        P("head", None, None),
        P("seq", None),
        P("seq", None),
    )
    out_specs = P("seq", "head")
    return jax.shard_map(body, mesh=mesh, in_specs=in_specs, out_specs=out_specs, check_vma=False)
```

profile of v0, /device:TPU:0, one launch (start us, length us, event | category | flops | bytes accessed | tf_op | source)
XLA Modules:
  0.0 304.3 jit_solution(13812923504323022759)
XLA Ops:
  6.5 0.8 reshape.301
  7.3 0.2 convert_reduce_fusion
  7.5 0.1 select_reduce_fusion
  7.6 0.7 all_to_all.13
  8.3 7.3 %all-to-all-start = ((s32[8,1,8]{2,1,0:T(1,128)}), s32[8,1,8]{2,1,0:T(1,128)S(1)}, u32[]{:S(2)}, u32[]{:S(2)}) async-start(s32[8,1,8]{2,1,0:T(1,128)} %bitcast.6), calls=%async_computation | async-start | bytes 8192 | tf_op jit(solution)/shard_map/all_to_all | solution.py:68
  15.6 14.1 %copy.49 = bf16[8192,576]{1,0:T(8,128)(2,1)} copy(bf16[8192,576]{0,1:T(8,128)(2,1)} %param.14) | data formatting | bytes 18874368 | tf_op args[5]
  29.7 2.0 constant_dynamic-slice_fusion
  31.6 0.0 all-to-all-done
  31.7 0.1 reshape.310
  31.8 2.4 gather_fusion
  34.1 0.0 copy-start.5
  34.1 3.6 %broadcast_select_fusion = bf16[8,8,32,576]{3,2,1,0:T(8,128)(2,1)} fusion(bf16[8,8,32,576]{3,2,1,0:T(8,128)(2,1)} %bitcast.53, pred[8,8]{1,0:T(8,128)(4,1)S(1)} %compare_and_fusion), kind=kLoop, calls=%fused_computation.22 | loop fusion | flops 1179648 | bytes 4718656 | tf_op jit(solution)/shard_map/jit(_take)/select_n | solution.py:69
  37.7 0.0 copy-start.4
  37.8 0.0 copy-start.3
  37.8 6.1 %all-to-all-start.1 = ((bf16[8,8,32,576]{3,2,1,0:T(8,128)(2,1)}), bf16[8,8,32,576]{3,2,1,0:T(8,128)(2,1)S(1)}, u32[]{:S(2)}, u32[]{:S(2)}) async-start(bf16[8,8,32,576]{3,2,1,0:T(8,128)(2,1)} %broadcast_select_fusion), calls=%async_computation.1 | async-start | bytes 5242880 | tf_op jit(solution)/shard_map/all_to_all | solution.py:70
  43.9 0.0 all-gather.3.cloned.1.call-start
  43.9 0.0 copy-done.5
  43.9 0.1 reshape.304
  44.0 58.8 %all-to-all-done.1 = bf16[8,8,32,576]{3,2,1,0:T(8,128)(2,1)S(1)} async-done(((bf16[8,8,32,576]{3,2,1,0:T(8,128)(2,1)}), bf16[8,8,32,576]{3,2,1,0:T(8,128)(2,1)S(1)}, u32[]{:S(2)}, u32[]{:S(2)}) %all-to-all-start.1) | async-done | bytes 2359328 | tf_op jit(solution)/shard_map/all_to_all | solution.py:70
  102.8 1.8 gather_fusion.1
  104.5 2.6 broadcast_select_fusion.1
  107.2 0.0 all-gather.3.cloned.1.call-update
  107.2 0.0 copy-done.4
  107.2 5.2 %all-gather = bf16[4,1,384]{2,1,0:T(2,128)(2,1)S(1)} all-gather(bf16[1,1,384]{2,1,0:T(2,128)(2,1)S(1)} %reshape.325), channel_id=1, replica_groups=mesh['seq'=8,'head'=4] {'head'}, dimensions={0}, use_global_device_ids=true | all-gather | bytes 3840 | tf_op jit(solution)/shard_map/all_gather | solution.py:51
  112.4 0.0 copy-done.3
  112.4 12.5 %all_gather.9 = bf16[256,1536]{1,0:T(8,128)(2,1)S(1)} all-gather(bf16[256,384]{1,0:T(8,128)(2,1)S(1)} %copy-done.3), channel_id=1, replica_groups=mesh['seq'=8,'head'=4] {'head'}, dimensions={1}, use_global_device_ids=true | all-gather | bytes 983040 | tf_op jit(solution)/shard_map/all_gather | solution.py:50
  124.9 0.2 fusion.17
  125.2 13.1 %convolution_convert_fusion = bf16[256,6144]{1,0:T(8,128)(2,1)} fusion(bf16[1536,6144]{1,0:T(8,128)(2,1)} %param.11, bf16[256,1536]{1,0:T(8,128)(2,1)S(1)} %all_gather.9, f32[1536]{0:T(1024)S(1)} %reshape.327, f32[256]{0:T(256)S(1)} %add_rsqrt_fusion), kind=kOutput, calls=%fused_computation.21 | convolution fusion | flops 4834983936 | bytes 22813696 | tf_op jit(solution)/shard_map/dot_general | solution.py:76
  138.2 3.2 %copy.43 = bf16[256,6144]{0,1:T(8,128)(2,1)S(1)} copy(bf16[256,6144]{1,0:T(8,128)(2,1)} %convolution_convert_fusion) | data formatting | bytes 6291456 | tf_op jit(solution)/shard_map/convert_element_type | solution.py:76
  141.5 0.2 multiply_cosine_fusion
  141.7 1.3 fusion.21
  143.0 2.7 copy.45
  145.7 2.6 copy.46
  148.3 0.0 copy-start.1
  148.3 0.0 copy-start.2
  148.3 4.8 %convert_bitcast_fusion = bf16[256,32,512]{2,0,1:T(8,128)(2,1)S(1)} fusion(bf16[32,128,512]{2,1,0:T(8,128)(2,1)} %param.12, bf16[256,32,192]{0,2,1:T(8,128)(2,1)S(1)} %bitcast.51), kind=kOutput, calls=%fused_computation.20 | convolution fusion | flops 1077936128 | bytes 14680064 | tf_op jit(solution)/shard_map/thn,hnl->thl/dot_general | solution.py:81
  153.1 0.0 copy-done.1
  153.1 0.0 copy-done.2
  153.1 12.0 %pad_maximum_fusion = bf16[256,32,576]{2,0,1:T(8,128)(2,1)} fusion(bf16[256,32,32]{2,0,1:T(8,128)(2,1)S(1)} %copy-done.2, bf16[256,32,32]{2,0,1:T(8,128)(2,1)S(1)} %copy-done.1, bf16[256,32,512]{2,0,1:T(8,128)(2,1)S(1)} %convert_bitcast_fusion), kind=kLoop, calls=%fused_computation.17 | loop fusion | flops 28311552 | bytes 18874368 | tf_op jit(solution)/shard_map/concatenate | solution.py:84
  165.1 14.0 %copy.47 = bf16[256,32,576]{2,1,0:T(8,128)(2,1)} copy(bf16[256,32,576]{2,0,1:T(8,128)(2,1)} %pad_maximum_fusion) | data formatting | bytes 18874368 | tf_op jit(solution)/shard_map/concatenate | solution.py:84
  179.1 0.0 all-gather.3.cloned.1.call-done
  179.1 105.8 %while.10 = (s32[]{:T(128)}, bf16[2,4096,512]{2,1,0:T(8,128)(2,1)}, bf16[2,4096,576]{2,1,0:T(8,128)(2,1)}, bf16[2,2048,576]{2,1,0:T(8,128)(2,1)}, s32[]{:T(128)}) while((s32[]{:T(128)}, bf16[2,4096,512]{2,1,0:T(8,128)(2,1)}, bf16[2,4096,576]{2,1,0:T(8,128)(2,1)}, bf16[2,2048,576]{2,1,0:T(8,128)(2,1)}, s32[]{:T(128)}) %tuple.31), condition=%wide.region_6.7_spmd, body=%wide.region_3.6_spmd.sunk | while | flops 18331197440 | bytes 138495600 | solution.py:102
  179.1 22.0 %multiply_reduce_fusion.2 = (f32[4096]{0:T(1024)S(1)}, f32[4096,2048]{0,1:T(8,128)}) fusion(bf16[2,2048,576]{2,1,0:T(8,128)(2,1)} %get-tuple-element.88, s32[]{:T(128)} %get-tuple-element.80, bf16[2,4096,576]{2,1,0:T(8,128)(2,1)} %get-tuple-element.87), kind=kOutput, calls=%fused_computation.4.clone.1 | convolution fusion | flops 9680449536 | bytes 41436160 | tf_op jit(solution)/shard_map/while/body/eval_jaxpr/dot_general | solution.py:92
  201.1 0.0 copy-start
  201.1 14.0 %fusion.36 = f32[4096]{0:T(1024)S(1)} fusion(f32[4096,2048]{0,1:T(8,128)} %get-tuple-element.73, f32[4096]{0:T(1024)S(1)} %get-tuple-element.74), kind=kLoop, calls=%fused_computation.5.clone.1 | loop fusion | flops 25161728 | bytes 33587200 | tf_op jit(solution)/shard_map/while/body/eval_jaxpr/reduce_sum | solution.py:97
  215.2 0.0 copy-done
  215.2 0.2 dynamic-slice_bitcast_fusion.3
  215.4 16.6 %fusion.37 = bf16[2,4096,512]{2,1,0:T(8,128)(2,1)} fusion(bf16[2,4096,512]{2,1,0:T(8,128)(2,1)} %get-tuple-element.81, s32[]{:T(128)} %get-tuple-element.80, f32[4096,2048]{0,1:T(8,128)} %get-tuple-element.73, f32[4096]{0:T(1024)S(1)} %fusion.36, f32[4096]{0:T(1024)S(1)} %get-tuple-element.74, bf16[2048,576]{1,0:T(8,128)(2,1)S(1)} %dynamic-slice_bitcast_fusion.3), kind=kOutput, calls=%fused_computation.9.clone.1 | convolution fusion | flops 8625586176 | bytes 39879168 | tf_op jit(solution)/shard_map/while/body/eval_jaxpr/dot_general | solution.py:98
  232.0 22.0 %multiply_reduce_fusion.2 = (f32[4096]{0:T(1024)S(1)}, f32[4096,2048]{0,1:T(8,128)}) fusion(bf16[2,2048,576]{2,1,0:T(8,128)(2,1)} %get-tuple-element.88, s32[]{:T(128)} %get-tuple-element.80, bf16[2,4096,576]{2,1,0:T(8,128)(2,1)} %get-tuple-element.87), kind=kOutput, calls=%fused_computation.4.clone.1 | convolution fusion | flops 9680449536 | bytes 41436160 | tf_op jit(solution)/shard_map/while/body/eval_jaxpr/dot_general | solution.py:92
  254.0 0.0 copy-start
  254.0 14.0 %fusion.36 = f32[4096]{0:T(1024)S(1)} fusion(f32[4096,2048]{0,1:T(8,128)} %get-tuple-element.73, f32[4096]{0:T(1024)S(1)} %get-tuple-element.74), kind=kLoop, calls=%fused_computation.5.clone.1 | loop fusion | flops 25161728 | bytes 33587200 | tf_op jit(solution)/shard_map/while/body/eval_jaxpr/reduce_sum | solution.py:97
  268.1 0.0 copy-done
  268.1 0.2 dynamic-slice_bitcast_fusion.3
  268.3 16.6 %fusion.37 = bf16[2,4096,512]{2,1,0:T(8,128)(2,1)} fusion(bf16[2,4096,512]{2,1,0:T(8,128)(2,1)} %get-tuple-element.81, s32[]{:T(128)} %get-tuple-element.80, f32[4096,2048]{0,1:T(8,128)} %get-tuple-element.73, f32[4096]{0:T(1024)S(1)} %fusion.36, f32[4096]{0:T(1024)S(1)} %get-tuple-element.74, bf16[2048,576]{1,0:T(8,128)(2,1)S(1)} %dynamic-slice_bitcast_fusion.3), kind=kOutput, calls=%fused_computation.9.clone.1 | convolution fusion | flops 8625586176 | bytes 39879168 | tf_op jit(solution)/shard_map/while/body/eval_jaxpr/dot_general | solution.py:98
  284.9 9.7 %fusion.14 = bf16[32,256,128]{1,2,0:T(8,128)(2,1)S(1)} fusion(bf16[32,512,128]{2,1,0:T(8,128)(2,1)} %param.13, bf16[256,32,512]{2,1,0:T(8,128)(2,1)} %bitcast.58), kind=kOutput, calls=%fused_computation.26 | convolution fusion | flops 1074790400 | bytes 14680064 | tf_op jit(solution)/shard_map/thl,hlv->thv/dot_general | solution.py:103
  294.6 2.9 copy.52
  (14 shorter events, 0.1 us)
Async XLA Ops:
  8.3 23.4 %all-to-all-start = ((s32[8,1,8]{2,1,0:T(1,128)}), s32[8,1,8]{2,1,0:T(1,128)S(1)}, u32[]{:S(2)}, u32[]{:S(2)}) async-start(s32[8,1,8]{2,1,0:T(1,128)} %bitcast.6), calls=%async_computation | async-start | bytes 8192 | tf_op jit(solution)/shard_map/all_to_all | solution.py:68
  34.1 9.8 %copy-start.5 = (s32[2,16]{1,0:T(2,128)S(1)}, s32[2,16]{1,0:T(2,128)}, u32[]{:S(2)}) copy-start(s32[2,16]{1,0:T(2,128)} %param.15) | copy-start | bytes 388
  37.7 69.4 %copy-start.4 = (bf16[384]{0:T(512)(128)(2,1)S(1)}, bf16[384]{0:T(512)(128)(2,1)}, u32[]{:S(2)}) copy-start(bf16[384]{0:T(512)(128)(2,1)} %param.10) | copy-start | bytes 2308
  37.8 74.7 %copy-start.3 = (bf16[256,384]{1,0:T(8,128)(2,1)S(1)}, bf16[256,384]{1,0:T(8,128)(2,1)}, u32[]{:S(2)}) copy-start(bf16[256,384]{1,0:T(8,128)(2,1)} %param.9) | copy-start | bytes 589828
  37.8 65.0 %all-to-all-start.1 = ((bf16[8,8,32,576]{3,2,1,0:T(8,128)(2,1)}), bf16[8,8,32,576]{3,2,1,0:T(8,128)(2,1)S(1)}, u32[]{:S(2)}, u32[]{:S(2)}) async-start(bf16[8,8,32,576]{3,2,1,0:T(8,128)(2,1)} %broadcast_select_fusion), calls=%async_computation.1 | async-start | bytes 5242880 | tf_op jit(solution)/shard_map/all_to_all | solution.py:70
  43.9 135.3 %all-gather.3.cloned.1.call-start = ((), (), s32[]{:S(2)}) async-start(), calls=%async_computation.2 | async-start | bytes 6553600 | tf_op jit(solution)/shard_map/all_gather | solution.py:73
  148.3 4.8 %copy-start.1 = (bf16[256,32,32]{2,0,1:T(8,128)(2,1)S(1)}, bf16[256,32,32]{2,0,1:T(8,128)(2,1)}, u32[]{:S(2)}) copy-start(bf16[256,32,32]{2,0,1:T(8,128)(2,1)} %copy.45) | copy-start | bytes 1572868
  148.3 4.8 %copy-start.2 = (bf16[256,32,32]{2,0,1:T(8,128)(2,1)S(1)}, bf16[256,32,32]{2,0,1:T(8,128)(2,1)}, u32[]{:S(2)}) copy-start(bf16[256,32,32]{2,0,1:T(8,128)(2,1)} %copy.46) | copy-start | bytes 1572868
  201.1 14.0 %copy-start = (bf16[2,2048,576]{2,1,0:T(8,128)(2,1)S(1)}, bf16[2,2048,576]{2,1,0:T(8,128)(2,1)}, u32[]{:S(2)}) copy-start(bf16[2,2048,576]{2,1,0:T(8,128)(2,1)} %get-tuple-element.88) | copy-start | bytes 14155780 | tf_op jit(solution)/shard_map/while
  254.0 14.0 %copy-start = (bf16[2,2048,576]{2,1,0:T(8,128)(2,1)S(1)}, bf16[2,2048,576]{2,1,0:T(8,128)(2,1)}, u32[]{:S(2)}) copy-start(bf16[2,2048,576]{2,1,0:T(8,128)(2,1)} %get-tuple-element.88) | copy-start | bytes 14155780 | tf_op jit(solution)/shard_map/while
Sparse Core Ops, SparseCore 0:
  107.3 42.6 all-gather.2
where the time goes:
time: 305 us; the launch traced here: 304 us
  matrix products  105 us (34%)
  waiting for transfers between devices  58.8 us (19%)
  other arithmetic  48.4 us (16%)
  local copies, waits for them, and re-layouts  47.7 us (16%)
  blocking collectives  17.7 us (6%)
  starting transfers between devices  13.5 us (4%)
  between operations  13.5 us (4%)
    all_to_all x1, waiting for transfers between devices, body(): lax.all_to_all(found, 'seq', split_axis=0, concat_axis=0, tiled=True)  58.8 us
    dot_general x2, matrix products, one_block(): lax.dot_general(block_q, block_keys, (((1,), (1,)), ((), ())), preferred_...  44 us
    dot_general x2, matrix products, one_block(): jnp.dot(weights, block_keys[:, :LATENT], preferred_element_type=jnp.float32)  33.2 us
    reduce_sum x2, other arithmetic, one_block(): weights = jax.nn.softmax(scores, axis=-1).astype(jnp.bfloat16)  28 us
    unnamed x12, local copies, waits for them, and re-layouts  14.1 us
    concatenate x1, local copies, waits for them, and re-layouts, body(): jnp.concatenate([latent_q, rotated], axis=-1)  14 us
    dot_general x1, matrix products, body(): jnp.dot(normed, q_up, preferred_element_type=jnp.float32)  13.1 us
    all_gather x1, blocking collectives, body(): lax.all_gather(q_low, 'head', axis=1, tiled=True)  12.5 us
  transfers between devices with their start and end apart: 3, of which 1 were waited for; matrix products, arithmetic and copies ran while one was open for 23% of the time, Pallas kernels for 0%

commit v1 on v0

v1 whole, which is shorter than its diff:
```python
import jax
import jax.numpy as jnp
from jax import lax
from jax.experimental import pallas as pl
from jax.experimental.pallas import tpu as pltpu
from jax.sharding import PartitionSpec as P

NOPE = 128
ROPE = 64
LATENT = 512
VDIM = 128
TILE = 128
TOPT = 16
QBLK = 128
LANES = 128
LOG2E = 1.4426950408889634


def rms_normed(q_low, q_gain):
    values = q_low.astype(jnp.float32)
    power = jnp.mean(values * values, axis=-1, keepdims=True)
    return (values * lax.rsqrt(power + 1e-06) * q_gain.astype(jnp.float32)).astype(jnp.bfloat16)


def rotary_tables(positions):
    half = ROPE // 2
    freq = jnp.power(
        jnp.float32(10000.0), -(2.0 * jnp.arange(half, dtype=jnp.float32)) / ROPE
    )
    angle = positions.astype(jnp.float32)[:, None] * freq[None, :]
    cosine, sine = jnp.cos(angle), jnp.sin(angle)
    return (
        jnp.concatenate([cosine, cosine], axis=-1),
        jnp.concatenate([-sine, sine], axis=-1),
    )


def absorb_kernel(query_ref, absorb_ref, cos_ref, sin_ref, out_ref):
    heads = absorb_ref.shape[0]
    rows = query_ref.shape[0]
    half = ROPE // 2
    cosine, sine = cos_ref[...], sin_ref[...]
    for head in range(heads):
        start = head * (NOPE + ROPE)
        nope = query_ref[:, start : start + NOPE]
        rope = query_ref[:, start + NOPE : start + NOPE + ROPE].astype(jnp.float32)
        swapped = jnp.concatenate([rope[:, half:], rope[:, :half]], axis=-1)
        rotated = rope * cosine + swapped * sine
        out_ref[head, :, :LATENT] = jnp.dot(
            nope, absorb_ref[head], preferred_element_type=jnp.float32
        ).astype(jnp.bfloat16)
        out_ref[head, :, LATENT:] = jnp.concatenate(
            [rotated, jnp.zeros((rows, LANES - ROPE), jnp.float32)], axis=-1
        ).astype(jnp.bfloat16)


def absorbed_query(query, key_absorb, cosine, sine):
    rows = query.shape[0]
    group = key_absorb.shape[0]
    step = min(8, group)
    width = LATENT + LANES
    return pl.pallas_call(
        absorb_kernel,
        grid=(group // step,),
        in_specs=[
            pl.BlockSpec((rows, step * (NOPE + ROPE)), lambda i: (0, i)),
            pl.BlockSpec((step, NOPE, LATENT), lambda i: (i, 0, 0)),
            pl.BlockSpec((rows, ROPE), lambda i: (0, 0)),
            pl.BlockSpec((rows, ROPE), lambda i: (0, 0)),
        ],
        out_specs=pl.BlockSpec((step, rows, width), lambda i: (i, 0, 0)),
        out_shape=jax.ShapeDtypeStruct((group, rows, width), jnp.bfloat16),
        cost_estimate=pl.CostEstimate(
            flops=2 * rows * group * NOPE * LATENT,
            bytes_accessed=2 * (query.size + key_absorb.size + group * rows * width),
            transcendentals=0,
        ),
        name="absorb",
    )(query, key_absorb, cosine, sine)


def attend_kernel(query_ref, keys_ref, absorb_ref, out_ref, turned, values):
    heads = absorb_ref.shape[0]
    tiles, width = keys_ref.shape[1:3]

    @pl.when(pl.program_id(1) == 0)
    def _():
        turned[width:, :] = jnp.zeros((turned.shape[0] - width, turned.shape[1]), turned.dtype)
        for tile in range(tiles):
            span = slice(tile * TILE, (tile + 1) * TILE)
            turned[:width, span] = keys_ref[0, tile]
            values[span, :] = keys_ref[0, tile, :LATENT, :].T

    scale = float(NOPE + ROPE) ** (-0.5) * LOG2E
    pair = 2
    scores = []
    for at in range(0, heads, pair):
        block = query_ref[at : at + pair].reshape(pair * QBLK, query_ref.shape[2])
        scores.append(
            jnp.dot(block, turned[...], preferred_element_type=jnp.float32)
        )
    for at in range(0, heads, pair):
        score = scores[at // pair]
        top = jnp.max(score, axis=-1, keepdims=True)
        weights = jnp.exp2((score - top) * scale)
        total = jnp.sum(weights, axis=-1, keepdims=True)
        mixed = jnp.dot(
            weights.astype(jnp.bfloat16),
            values[...],
            preferred_element_type=jnp.float32,
        )
        mixed = (mixed / total).astype(jnp.bfloat16)
        for head in range(pair):
            out_ref[:, (at + head) * VDIM : (at + head + 1) * VDIM] = jnp.dot(
                mixed[head * QBLK : (head + 1) * QBLK],
                absorb_ref[at + head],
                preferred_element_type=jnp.float32,
            ).astype(jnp.bfloat16)


def attend(full_q, keys, value_absorb):
    group, rows, padded = full_q.shape
    blocks, tiles, width = keys.shape[:3]
    count = tiles * TILE
    step = min(4, group)
    return pl.pallas_call(
        attend_kernel,
        grid=(blocks, group // step),
        in_specs=[
            pl.BlockSpec((step, QBLK, padded), lambda b, g: (g, b, 0)),
            pl.BlockSpec((1, tiles, width, TILE), lambda b, g: (b, 0, 0, 0)),
            pl.BlockSpec((step, LATENT, VDIM), lambda b, g: (g, 0, 0)),
        ],
        out_specs=pl.BlockSpec((QBLK, step * VDIM), lambda b, g: (b, g)),
        out_shape=jax.ShapeDtypeStruct((rows, group * VDIM), jnp.bfloat16),
        scratch_shapes=[
            pltpu.VMEM((padded, count), jnp.bfloat16),
            pltpu.VMEM((count, LATENT), jnp.bfloat16),
        ],
        compiler_params=pltpu.CompilerParams(
            dimension_semantics=("arbitrary", "arbitrary"), vmem_limit_bytes=60 * 1024 * 1024
        ),
        cost_estimate=pl.CostEstimate(
            flops=2 * rows * group * count * (padded + LATENT),
            bytes_accessed=2 * (full_q.size + keys.size + value_absorb.size * blocks),
            transcendentals=rows * group * count,
        ),
        name="attend",
    )(full_q, keys, value_absorb)


def owner_rank(picks, tiles_dev):
    owner = picks // tiles_dev
    order = jnp.arange(picks.shape[0], dtype=jnp.int32)
    same = picks[:, None] == picks[None, :]
    first = jnp.min(jnp.where(same, order[None, :], picks.shape[0]), axis=1)
    fresh = first == order
    before = (owner[:, None] == owner[None, :]) & fresh[None, :] & (order[None, :] < first[:, None])
    return (owner, jnp.sum(before.astype(jnp.int32), axis=1), fresh)


def place_table(place, local, length):
    hit = place[:, None] == jnp.arange(length, dtype=jnp.int32)[None, :]
    return jnp.sum(jnp.where(hit, local[:, None], 0), axis=0)


def body(q_low, q_gain, q_up, key_absorb, value_absorb, latent_cache, tile_picks):
    whole_low, whole_gain = (
        lax.all_gather(q_low, "head", axis=1, tiled=True),
        lax.all_gather(q_gain, "head", axis=0, tiled=True),
    )
    rows = whole_low.shape[0]
    width = latent_cache.shape[1]
    seq_count = lax.axis_size("seq")
    tiles_dev = latent_cache.shape[0] // TILE
    picks = tile_picks.reshape(-1)
    count = picks.shape[0]
    cap = max(2, 2 * count // seq_count)
    owner, rank, fresh = owner_rank(picks, tiles_dev)
    share = width // lax.axis_size("head")
    columns = lax.dynamic_slice_in_dim(latent_cache, lax.axis_index("head") * share, share, 1)
    cache_tiles = columns.T.reshape(share, tiles_dev, TILE).transpose(1, 0, 2)
    requests = place_table(
        owner * cap + rank, jnp.where(fresh, picks % tiles_dev, 0), seq_count * cap
    ).reshape(
        seq_count, cap
    )
    serve_requests = lax.all_to_all(requests, "seq", split_axis=0, concat_axis=0, tiled=True)
    found = jnp.take(cache_tiles, serve_requests, axis=0, mode="clip")
    fetched = lax.all_to_all(found, "seq", split_axis=0, concat_axis=0, tiled=True)
    flat = fetched.reshape(seq_count * cap, share, TILE)
    keys = jnp.take(flat, owner * cap + rank, axis=0, mode="clip")
    normed = rms_normed(whole_low, whole_gain)
    query = jnp.dot(normed, q_up, preferred_element_type=jnp.float32).astype(jnp.bfloat16)
    keys, query = lax.optimization_barrier((keys, query))
    keys = lax.all_gather(keys, "head", axis=1, tiled=True)
    keys = keys.reshape(count // TOPT, TOPT, width, TILE)
    context = latent_cache.shape[0] * seq_count
    positions = context + lax.axis_index("seq") * rows + jnp.arange(rows, dtype=jnp.int32)
    full_q = absorbed_query(query, key_absorb, *rotary_tables(positions))
    return attend(full_q, keys, value_absorb)


def solution(mesh):
    in_specs = (
        P("seq", "head"),
        P("head"),
        P(None, "head"),
        P("head", None, None),
        P("head", None, None),
        P("seq", None),
        P("seq", None),
    )
    out_specs = P("seq", "head")
    return jax.shard_map(body, mesh=mesh, in_specs=in_specs, out_specs=out_specs, check_vma=False)
```

time: 305 us -> 189 us (0.62)
  matrix products: 105 us -> 13 us
  Pallas kernels: 0 us -> 71 us
  other arithmetic: 48.4 us -> 2.84 us
  local copies, waits for them, and re-layouts: 47.7 us -> 8.19 us
  blocking collectives: 17.7 us -> 13.9 us
  waiting for transfers between devices: 58.8 us -> 55.1 us
    dot_general x6 -> x0, matrix products: 91.7 us -> none  [the longest x2 44 us: one_block(): lax.dot_general(block_q, block_keys, (((1,), (1,)), ((), ())), preferred_...]
    pallas_call x0 -> x2, Pallas kernels: none -> 71 us  [the longest x1 61.2 us: attend(): pl.pallas_call(attend_kernel, grid=(blocks, group // step), in_specs=[pl....]
    all_to_all x1, waiting for transfers between devices: 58.8 us -> 25.3 us  [body(): lax.all_to_all(found, 'seq', split_axis=0, concat_axis=0, tiled=True)]
    reduce_sum x3 -> x1, other arithmetic: 28.2 us -> 0.18 us  [owner_rank(): return (owner, jnp.sum(before.astype(jnp.int32), axis=1), fresh)]
    all_gather x1, waiting for transfers between devices: 0.01 us -> 25.4 us  [body(): keys = lax.all_gather(keys, 'head', axis=1, tiled=True)]
    unnamed x12 -> x7, local copies, waits for them, and re-layouts: 14.1 us -> 0.02 us
    concatenate x1 -> x0, local copies, waits for them, and re-layouts: 14 us -> none  [body(): jnp.concatenate([latent_q, rotated], axis=-1)]
    concatenate x1, other arithmetic: 12 us -> 0.85 us  [rotary_tables(): jnp.concatenate([cosine, cosine], axis=-1)]
  transfers between devices with their start and end apart: 3 -> 3, of which waited for: 1 -> 3; matrix products, arithmetic and copies ran while one was open for 23% -> 9% of each run, Pallas kernels for 0% -> 5%
where the time goes in v1:
time: 189 us
  Pallas kernels  71 us (38%)
  waiting for transfers between devices  55.1 us (29%)
  blocking collectives  13.9 us (7%)
  between operations  13.5 us (7%)
  matrix products  13 us (7%)
  starting transfers between devices  11.1 us (6%)
  local copies, waits for them, and re-layouts  8.19 us (4%)
  other arithmetic  2.84 us (2%)
    pallas_call x1, Pallas kernels, attend(): pl.pallas_call(attend_kernel, grid=(blocks, group // step), in_specs=[pl....  61.2 us
    all_gather x1, waiting for transfers between devices, body(): keys = lax.all_gather(keys, 'head', axis=1, tiled=True)  25.4 us
    all_to_all x1, waiting for transfers between devices, body(): lax.all_to_all(found, 'seq', split_axis=0, concat_axis=0, tiled=True)  25.3 us
    dot_general x1, matrix products, body(): jnp.dot(normed, q_up, preferred_element_type=jnp.float32)  13 us
    pallas_call x1, Pallas kernels, absorbed_query(): pl.pallas_call(absorb_kernel, grid=(group // step,), in_specs=[pl.BlockSp...  9.74 us
    all_gather x1, blocking collectives, body(): lax.all_gather(q_low, 'head', axis=1, tiled=True)  8.71 us
    all_to_all x1, starting transfers between devices, body(): lax.all_to_all(requests, 'seq', split_axis=0, concat_axis=0, tiled=True)  7.31 us
    all_gather x1, blocking collectives, body(): lax.all_gather(q_gain, 'head', axis=0, tiled=True)  5.16 us
  transfers between devices with their start and end apart: 3, of which 3 were waited for; matrix products, arithmetic and copies ran while one was open for 9% of the time, Pallas kernels for 5%

profile of v1, /device:TPU:0, one launch (start us, length us, event | category | flops | bytes accessed | tf_op | source)
XLA Modules:
  0.0 188.6 jit_solution(5399454564548222869)
XLA Ops:
  6.5 0.8 reshape.199
  7.3 0.2 select_reduce_fusion.1
  7.5 0.2 convert_reduce_fusion
  7.7 0.1 select_reduce_fusion
  7.8 0.7 all_to_all.9
  8.5 7.3 %all-to-all-start = ((s32[8,1,8]{2,1,0:T(1,128)}), s32[8,1,8]{2,1,0:T(1,128)S(1)}, u32[]{:S(2)}, u32[]{:S(2)}) async-start(s32[8,1,8]{2,1,0:T(1,128)} %bitcast.2), calls=%async_computation | async-start | bytes 8192 | tf_op jit(solution)/shard_map/all_to_all | solution.py:188
  15.8 2.1 %bitcast_bitcast_fusion = bf16[64,144,128]{2,1,0:T(8,128)(2,1)S(1)} fusion(bf16[8192,576]{0,1:T(8,128)(2,1)} %param.12, s32[]{:T(128)S(6)} %select_n.52), kind=kLoop, calls=%fused_computation.3 | loop fusion | bytes 4718596 | tf_op jit(solution)/shard_map/transpose | solution.py:182
  17.9 4.3 %all-to-all-done = s32[8,1,8]{2,1,0:T(1,128)S(1)} async-done(((s32[8,1,8]{2,1,0:T(1,128)}), s32[8,1,8]{2,1,0:T(1,128)S(1)}, u32[]{:S(2)}, u32[]{:S(2)}) %all-to-all-start) | async-done | bytes 288 | tf_op jit(solution)/shard_map/all_to_all | solution.py:188
  22.2 0.5 broadcast.203
  22.7 0.7 reduce.5
  23.4 0.1 reshape.205
  23.5 2.3 %gather_fusion = bf16[64,144,128]{2,1,0:T(8,128)(2,1)} fusion(bf16[64,144,128]{2,1,0:T(8,128)(2,1)S(1)} %bitcast_bitcast_fusion, s32[1024]{0:T(1024)S(1)} %pad_clamp_fusion.1), kind=kCustom, calls=%fused_computation | custom fusion | bytes 4718848 | tf_op jit(solution)/shard_map/jit(_take)/gather | solution.py:189
  25.7 0.0 copy-start.2
  25.7 0.0 copy-start.1
  25.7 0.0 copy-start
  25.7 3.7 %all-to-all-start.1 = ((bf16[8,8,144,128]{3,2,1,0:T(8,128)(2,1)}), bf16[8,8,144,128]{3,2,1,0:T(8,128)(2,1)S(1)}, u32[]{:S(2)}, u32[]{:S(2)}) async-start(bf16[8,8,144,128]{3,2,1,0:T(8,128)(2,1)} %bitcast.3), calls=%async_computation.1 | async-start | bytes 4718592 | tf_op jit(solution)/shard_map/all_to_all | solution.py:190
  29.5 0.0 all-gather.3.cloned.1.call-start
  29.5 0.0 copy-done.2
  29.6 0.1 reshape.201
  29.6 0.0 copy-done.1
  29.6 5.2 %all-gather = bf16[4,1,384]{2,1,0:T(2,128)(2,1)S(1)} all-gather(bf16[1,1,384]{2,1,0:T(2,128)(2,1)S(1)} %reshape.221), channel_id=1, replica_groups=mesh['seq'=8,'head'=4] {'head'}, dimensions={0}, use_global_device_ids=true | all-gather | bytes 3840 | tf_op jit(solution)/shard_map/all_gather | solution.py:170
  34.9 0.0 copy-done
  34.9 8.7 %all_gather.9 = bf16[256,1536]{1,0:T(8,128)(2,1)S(1)} all-gather(bf16[256,384]{1,0:T(8,128)(2,1)S(1)} %copy-done), channel_id=1, replica_groups=mesh['seq'=8,'head'=4] {'head'}, dimensions={1}, use_global_device_ids=true | all-gather | bytes 983040 | tf_op jit(solution)/shard_map/all_gather | solution.py:169
  43.6 0.2 fusion
  43.8 13.0 %convolution_convert_fusion.query_ref = bf16[256,6144]{1,0:T(8,128)(2,1)} fusion(bf16[1536,6144]{1,0:T(8,128)(2,1)} %param.9, bf16[256,1536]{1,0:T(8,128)(2,1)S(1)} %all_gather.9, f32[1536]{0:T(1024)S(1)} %reshape.223, f32[256]{0:T(256)S(1)} %add_rsqrt_fusion), kind=kOutput, calls=%fused_computation.2 | convolution fusion | flops 4834983936 | bytes 22813696 | tf_op jit(solution)/shard_map/dot_general | solution.py:194
  56.9 25.3 %all-to-all-done.1 = bf16[8,8,144,128]{3,2,1,0:T(8,128)(2,1)S(1)} async-done(((bf16[8,8,144,128]{3,2,1,0:T(8,128)(2,1)}), bf16[8,8,144,128]{3,2,1,0:T(8,128)(2,1)S(1)}, u32[]{:S(2)}, u32[]{:S(2)}) %all-to-all-start.1) | async-done | bytes 2359328 | tf_op jit(solution)/shard_map/all_to_all | solution.py:190
  82.1 1.7 gather_fusion.1
  83.8 0.0 all-gather.3.cloned.1.call-update
  83.9 0.5 fusion.6
  84.4 0.9 pad_maximum_fusion
  85.3 9.7 %absorb.1.query_ref = bf16[32,256,640]{2,1,0:T(8,128)(2,1)} custom-call(bf16[256,6144]{1,0:T(8,128)(2,1)} %convolution_convert_fusion.query_ref, bf16[32,128,512]{2,1,0:T(8,128)(2,1)} %absorb_ref.2, f32[256,64]{1,0:T(8,128)} %get-tuple-element.14.cos_ref, f32[256,64]{1,0:T(8,128)} %get-tuple-element.15.sin_ref), custom_call_target="tpu_custom_call" | custom-call | flops 1073741824 | bytes 17825792 | tf_op jit(solution)/shard_map/absorb/pallas_call | solution.py:62
  95.0 25.4 %all-gather.3.cloned.1.call-done = bf16[32,576,128]{2,1,0:T(8,128)(2,1)} async-done(((bf16[32,144,128]{2,1,0:T(8,128)(2,1)}), bf16[32,576,128]{2,1,0:T(8,128)(2,1)}) %all-gather.3.cloned.1.call-update) | async-done | bytes 4718608 | tf_op jit(solution)/shard_map/all_gather | solution.py:196
  120.5 61.2 %attend.1 = bf16[256,4096]{1,0:T(8,128)(2,1)} custom-call(bf16[32,256,640]{2,1,0:T(8,128)(2,1)} %absorb.1.query_ref, bf16[2,16,576,128]{3,2,1,0:T(8,128)(2,1)} %bitcast.20, bf16[32,512,128]{2,1,0:T(8,128)(2,1)} %absorb_ref.3), custom_call_target="tpu_custom_call" | custom-call | flops 38654705664 | bytes 23592960 | tf_op jit(solution)/shard_map/attend/pallas_call | solution.py:126
  (12 shorter events, 0.1 us)
Async XLA Ops:
  8.5 13.7 %all-to-all-start = ((s32[8,1,8]{2,1,0:T(1,128)}), s32[8,1,8]{2,1,0:T(1,128)S(1)}, u32[]{:S(2)}, u32[]{:S(2)}) async-start(s32[8,1,8]{2,1,0:T(1,128)} %bitcast.2), calls=%async_computation | async-start | bytes 8192 | tf_op jit(solution)/shard_map/all_to_all | solution.py:188
  25.7 3.8 %copy-start.2 = (s32[2,16]{1,0:T(2,128)S(1)}, s32[2,16]{1,0:T(2,128)}, u32[]{:S(2)}) copy-start(s32[2,16]{1,0:T(2,128)} %param.13) | copy-start | bytes 388
  25.7 3.9 %copy-start.1 = (bf16[384]{0:T(512)(128)(2,1)S(1)}, bf16[384]{0:T(512)(128)(2,1)}, u32[]{:S(2)}) copy-start(bf16[384]{0:T(512)(128)(2,1)} %param.8) | copy-start | bytes 2308
  25.7 9.1 %copy-start = (bf16[256,384]{1,0:T(8,128)(2,1)S(1)}, bf16[256,384]{1,0:T(8,128)(2,1)}, u32[]{:S(2)}) copy-start(bf16[256,384]{1,0:T(8,128)(2,1)} %param.7) | copy-start | bytes 589828
  25.7 56.4 %all-to-all-start.1 = ((bf16[8,8,144,128]{3,2,1,0:T(8,128)(2,1)}), bf16[8,8,144,128]{3,2,1,0:T(8,128)(2,1)S(1)}, u32[]{:S(2)}, u32[]{:S(2)}) async-start(bf16[8,8,144,128]{3,2,1,0:T(8,128)(2,1)} %bitcast.3), calls=%async_computation.1 | async-start | bytes 4718592 | tf_op jit(solution)/shard_map/all_to_all | solution.py:190
  29.5 91.0 %all-gather.3.cloned.1.call-start = ((), (), s32[]{:S(2)}) async-start(), calls=%async_computation.2 | async-start | bytes 5898240 | tf_op jit(solution)/shard_map/all_gather | solution.py:196
Sparse Core Ops, SparseCore 0:
  84.0 36.4 all-gather.2
